TPU v7x, 32 devices: a whole 2x2x4 slice. The times are simulated.
32 devices in a mesh: blk: 8 (over z, x), bfly: 4 (over y, core).
Axes of the slice: x: 2, y: 2, z: 4, core: 2. Of those that a mesh axis runs over, the one named last changes fastest.
Arguments:
- port_vectors: bfloat16 [8, 4, 768, 128], P('blk', 'bfly'), may hold values from -6 to 6
- column_leaf: bfloat16 [8, 4, 384, 768], P('blk', 'bfly'), may hold values from -0.21875 to 0.21875
- transfer: bfloat16 [8, 4, 4, 384, 768], P('blk', None, 'bfly'), may hold values from -0.21875 to 0.21875
- row_leaf: bfloat16 [8, 4, 768, 384], P('blk', 'bfly'), may hold values from -0.3125 to 0.3125
Outputs:
- field: bfloat16 [4, 768, 128], P('bfly', 'blk')
All inputs are finite; a program needn't handle non-finite values.
Results may differ from a plain program's by a relative error of at most 0.0095.
Values may be sent and summed in bfloat16 or wider, within the bound.
A program may use at most 64 MiB of HBM per device.

v0:
```python
import math

import jax
import jax.numpy as jnp
from jax import lax
from jax.sharding import PartitionSpec as P


def from_partner(array, axis, bit):
    return lax.ppermute(array, axis, [(i, i ^ 1 << bit) for i in range(lax.axis_size(axis))])


def local(port_vectors, column_leaf, transfer, row_leaf):
    rank_rows = column_leaf.shape[2]
    bit_count = lax.axis_size("bfly").bit_length() - 1
    position = lax.axis_index("bfly")
    state = jnp.dot(
        column_leaf[0, 0], port_vectors[0, 0], preferred_element_type=jnp.float32
    ).astype(jnp.bfloat16)
    for level in range(transfer.shape[1]):
        bit = level % bit_count
        partner_state = from_partner(state, "bfly", bit)
        mine_low = position // 2**bit % 2 == 0
        lower = jnp.where(mine_low, state, partner_state)
        upper = jnp.where(mine_low, partner_state, state)
        matrix = transfer[0, level, 0]
        mixed = jnp.dot(matrix[:, :rank_rows], lower, preferred_element_type=jnp.float32)
        mixed = mixed + jnp.dot(matrix[:, rank_rows:], upper, preferred_element_type=jnp.float32)
        state = mixed.astype(jnp.bfloat16)
    leaf_rows = row_leaf[0, 0]
    owned = leaf_rows.shape[0] // lax.axis_size("blk")
    partial_rows = jnp.dot(leaf_rows, state, preferred_element_type=jnp.float32)
    summed = lax.psum_scatter(partial_rows, "blk", scatter_dimension=0, tiled=True)
    scaled = summed * (1.0 / math.sqrt(lax.axis_size("blk")))
    return scaled.astype(jnp.bfloat16).reshape(1, owned, scaled.shape[1])


def solution(mesh):
    placed = (
        P("blk", "bfly", None, None),
        P("blk", "bfly", None, None),
        P("blk", None, "bfly", None, None),
        P("blk", "bfly", None, None),
    )
    return jax.shard_map(
        local, mesh=mesh, in_specs=placed, out_specs=P("bfly", "blk", None), check_vma=False
    )
```

profile of v0, /device:TPU:0, one launch (start us, length us, event | category | flops | bytes accessed | tf_op | source)
XLA Modules:
  0.0 98.3 jit_solution(1919317549830046300)
XLA Ops:
  6.5 0.0 copy-start
  6.5 1.5 %convolution_convert_fusion = bf16[384,128]{1,0:T(8,128)(2,1)S(1)} fusion(bf16[1,1,384,768]{3,2,1,0:T(8,128)(2,1)} %param.5, bf16[1,1,768,128]{3,2,1,0:T(8,128)(2,1)} %param.4), kind=kOutput, calls=%fused_computation.9 | convolution fusion | flops 75546624 | bytes 884736 | tf_op jit(solution)/shard_map/dot_general | solution.py:17
  8.0 0.6 collective-permute-start
  8.6 1.8 %slice_bitcast_fusion.3 = (bf16[384,768]{1,0:T(8,128)(2,1)S(1)}, bf16[384,768]{1,0:T(8,128)(2,1)S(1)}, bf16[384,768]{1,0:T(8,128)(2,1)S(1)}, bf16[384,768]{1,0:T(8,128)(2,1)S(1)}) fusion(bf16[1,4,1,384,768]{4,3,2,1,0:T(8,128)(2,1)} %param.6), kind=kLoop, calls=%fused_computation.18 | loop fusion | bytes 4718592 | tf_op jit(solution)/shard_map/squeeze | solution.py:26
  10.4 0.0 collective-permute-done
  10.4 0.3 fusion.19
  10.6 0.3 fusion.6
  10.9 2.6 %collective-permute-start.1 = (bf16[384,128]{0,1:T(8,128)(2,1)S(1)}, bf16[384,128]{0,1:T(8,128)(2,1)S(1)}, u32[]{:S(2)}, u32[]{:S(2)}) collective-permute-start(bf16[384,128]{0,1:T(8,128)(2,1)S(1)} %fusion.6), channel_id=1, source_target_pairs={{0,2},{1,3},{2,0},{3,1},{4,6},{5,7},{6,4},{7,5},{8,10},{9,11},{10,... | collective-permute-start | bytes 294920 | tf_op jit(solution)/shard_map/ppermute | solution.py:10
  13.5 3.5 %collective-permute-done.1 = bf16[384,128]{0,1:T(8,128)(2,1)S(1)} collective-permute-done((bf16[384,128]{0,1:T(8,128)(2,1)S(1)}, bf16[384,128]{0,1:T(8,128)(2,1)S(1)}, u32[]{:S(2)}, u32[]{:S(2)}) %collective-permute-start.1) | collective-permute-done | bytes 98336 | tf_op jit(solution)/shard_map/ppermute | solution.py:10
  16.9 0.3 fusion.16
  17.2 0.3 fusion.5
  17.5 0.1 collective-permute-start.2
  17.6 1.3 %collective-permute-done.2 = bf16[384,128]{1,0:T(8,128)(2,1)S(1)} collective-permute-done((bf16[384,128]{1,0:T(8,128)(2,1)S(1)}, bf16[384,128]{1,0:T(8,128)(2,1)S(1)}, u32[]{:S(2)}, u32[]{:S(2)}) %collective-permute-start.2) | collective-permute-done | bytes 98336 | tf_op jit(solution)/shard_map/ppermute | solution.py:10
  18.8 0.3 fusion.13
  19.1 0.3 fusion.4
  19.4 1.8 %collective-permute-start.3 = (bf16[384,128]{0,1:T(8,128)(2,1)S(1)}, bf16[384,128]{0,1:T(8,128)(2,1)S(1)}, u32[]{:S(2)}, u32[]{:S(2)}) collective-permute-start(bf16[384,128]{0,1:T(8,128)(2,1)S(1)} %fusion.4), channel_id=1, source_target_pairs={{0,2},{1,3},{2,0},{3,1},{4,6},{5,7},{6,4},{7,5},{8,10},{9,11},{10,... | collective-permute-start | bytes 294920 | tf_op jit(solution)/shard_map/ppermute | solution.py:10
  21.2 3.1 %collective-permute-done.3 = bf16[384,128]{0,1:T(8,128)(2,1)S(1)} collective-permute-done((bf16[384,128]{0,1:T(8,128)(2,1)S(1)}, bf16[384,128]{0,1:T(8,128)(2,1)S(1)}, u32[]{:S(2)}, u32[]{:S(2)}) %collective-permute-start.3) | collective-permute-done | bytes 98336 | tf_op jit(solution)/shard_map/ppermute | solution.py:10
  24.3 0.2 fusion.9
  24.5 0.5 convolution_bitcast_fusion
  25.1 0.9 copy.13
  26.0 0.0 reduce-scatter.4.cloned.1.call-update
  26.0 63.8 %reduce-scatter.4.cloned.1.call-done = f32[96,128]{1,0:T(8,128)} async-done(((f32[768,128]{1,0:T(8,128)}), f32[96,128]{1,0:T(8,128)}) %reduce-scatter.4.cloned.1.call-update) | async-done | bytes 49168
  89.9 0.9 copy.14
  90.8 0.7 copy.10
  (3 shorter events, 0.0 us)
Async XLA Ops:
  6.5 18.0 %copy-start = (bf16[1,1,768,384]{3,2,1,0:T(8,128)(2,1)S(1)}, bf16[1,1,768,384]{3,2,1,0:T(8,128)(2,1)}, u32[]{:S(2)}) copy-start(bf16[1,1,768,384]{3,2,1,0:T(8,128)(2,1)} %param.7) | copy-start | bytes 1769476
  6.5 83.3 %reduce-scatter.4.cloned.1.call-start = ((), (), s32[]{:S(2)}) async-start(), calls=%async_computation.1 | async-start | bytes 442368
  8.0 2.3 %collective-permute-start = (bf16[384,128]{1,0:T(8,128)(2,1)S(1)}, bf16[384,128]{1,0:T(8,128)(2,1)S(1)}, u32[]{:S(2)}, u32[]{:S(2)}) collective-permute-start(bf16[384,128]{1,0:T(8,128)(2,1)S(1)} %convolution_convert_fusion), channel_id=1, source_target_pairs={{0,1},{1,0},{2,3},{3,2},{4,5},{5,4},{6,7},{7,6},{8,9},{9,8},{10,11... | collective-permute-start | bytes 294920 | tf_op jit(solution)/shard_map/ppermute | solution.py:10
  10.9 6.0 %collective-permute-start.1 = (bf16[384,128]{0,1:T(8,128)(2,1)S(1)}, bf16[384,128]{0,1:T(8,128)(2,1)S(1)}, u32[]{:S(2)}, u32[]{:S(2)}) collective-permute-start(bf16[384,128]{0,1:T(8,128)(2,1)S(1)} %fusion.6), channel_id=1, source_target_pairs={{0,2},{1,3},{2,0},{3,1},{4,6},{5,7},{6,4},{7,5},{8,10},{9,11},{10,... | collective-permute-start | bytes 294920 | tf_op jit(solution)/shard_map/ppermute | solution.py:10
  17.5 1.4 %collective-permute-start.2 = (bf16[384,128]{1,0:T(8,128)(2,1)S(1)}, bf16[384,128]{1,0:T(8,128)(2,1)S(1)}, u32[]{:S(2)}, u32[]{:S(2)}) collective-permute-start(bf16[384,128]{1,0:T(8,128)(2,1)S(1)} %fusion.5), channel_id=1, source_target_pairs={{0,1},{1,0},{2,3},{3,2},{4,5},{5,4},{6,7},{7,6},{8,9},{9,8},{10,11... | collective-permute-start | bytes 294920 | tf_op jit(solution)/shard_map/ppermute | solution.py:10
  19.4 4.9 %collective-permute-start.3 = (bf16[384,128]{0,1:T(8,128)(2,1)S(1)}, bf16[384,128]{0,1:T(8,128)(2,1)S(1)}, u32[]{:S(2)}, u32[]{:S(2)}) collective-permute-start(bf16[384,128]{0,1:T(8,128)(2,1)S(1)} %fusion.4), channel_id=1, source_target_pairs={{0,2},{1,3},{2,0},{3,1},{4,6},{5,7},{6,4},{7,5},{8,10},{9,11},{10,... | collective-permute-start | bytes 294920 | tf_op jit(solution)/shard_map/ppermute | solution.py:10
Sparse Core Ops, SparseCore 0:
  26.2 63.6 reduce-scatter.3
where the time goes:
time: 98.6 us; the launch traced here: 98.3 us
  waiting for transfers between devices  71.7 us (73%)
  between operations  13.5 us (14%)
  starting transfers between devices  5.02 us (5%)
  local copies, waits for them, and re-layouts  4.27 us (4%)
  matrix products  3.82 us (4%)
    unnamed x2, waiting for transfers between devices  63.9 us
    ppermute x4, waiting for transfers between devices, from_partner(): lax.ppermute(array, axis, [(i, i ^ 1 << bit) for i in range(lax.axis_size...  7.86 us
    ppermute x4, starting transfers between devices, from_partner(): lax.ppermute(array, axis, [(i, i ^ 1 << bit) for i in range(lax.axis_size...  5.02 us
  transfers between devices with their start and end apart: 5, of which 4 were waited for; matrix products, arithmetic and copies ran while one was open for 2% of the time, Pallas kernels for 0%

commit v1 on v0

v1 whole, which is shorter than its diff:
```python
import functools
import math

import jax
import jax.numpy as jnp
from jax import lax
from jax.experimental import pallas as pl
from jax.experimental.pallas import tpu as pltpu
from jax.sharding import PartitionSpec as P

MESH = pl.DeviceIdType.MESH


def kernel(
    n_blk, n_bfly,
    ports_hbm, column_hbm, transfer_hbm, row_hbm, out_ref,
    ports, column, transfer, row, stacked, outgoing, incoming,
    load_sem, send_sem, recv_sem, scatter_sem, gather_sem,
):
    levels, rank, _ = transfer.shape
    owned = outgoing.shape[1]
    bit_count = n_bfly.bit_length() - 1
    block = lax.axis_index("blk")
    position = lax.axis_index("bfly")

    loads = [
        pltpu.make_async_copy(ports_hbm.at[0, 0], ports, load_sem.at[0]),
        pltpu.make_async_copy(column_hbm.at[0, 0], column, load_sem.at[1]),
    ]
    for level in range(levels):
        loads.append(
            pltpu.make_async_copy(
                transfer_hbm.at[0, level, 0], transfer.at[level], load_sem.at[2 + level]
            )
        )
    loads.append(pltpu.make_async_copy(row_hbm.at[0, 0], row, load_sem.at[2 + levels]))
    for load in loads:
        load.start()

    bits = [(position // 2**bit) % 2 for bit in range(bit_count)]
    partners = [position + (1 - 2 * bits[bit]) * 2**bit for bit in range(bit_count)]
    barrier = pltpu.get_barrier_semaphore()
    for bit in range(min(bit_count, levels)):
        pl.semaphore_signal(
            barrier, inc=1, device_id={"bfly": partners[bit]}, device_id_type=MESH
        )
    for step in range(1, n_blk):
        pl.semaphore_signal(
            barrier, inc=1, device_id={"blk": lax.rem(block + step, n_blk)}, device_id_type=MESH
        )

    loads[0].wait()
    loads[1].wait()
    state = jnp.dot(column[...], ports[...], preferred_element_type=jnp.float32)
    pl.semaphore_wait(barrier, min(bit_count, levels) + n_blk - 1)

    sends = []
    for level in range(levels):
        bit = level % bit_count
        mine = pl.ds(pl.multiple_of(bits[bit] * rank, rank), rank)
        other = pl.ds(pl.multiple_of((1 - bits[bit]) * rank, rank), rank)
        stacked[level, mine, :] = state.astype(jnp.bfloat16)
        copy = pltpu.make_async_remote_copy(
            src_ref=stacked.at[level, mine, :],
            dst_ref=stacked.at[level, mine, :],
            send_sem=send_sem.at[level],
            recv_sem=recv_sem.at[level],
            device_id={"bfly": partners[bit]},
            device_id_type=MESH,
        )
        copy.start()
        sends.append(copy)
        loads[2 + level].wait()
        state = jnp.dot(
            transfer[level, :, mine], stacked[level, mine, :],
            preferred_element_type=jnp.float32,
        )
        copy.wait_recv()
        state = state + jnp.dot(
            transfer[level, :, other], stacked[level, other, :],
            preferred_element_type=jnp.float32,
        )

    loads[2 + levels].wait()
    state = state.astype(jnp.bfloat16)
    partial = jnp.dot(row[...], state, preferred_element_type=jnp.float32)
    for index in range(n_blk):
        outgoing[index] = partial[index * owned : (index + 1) * owned].astype(jnp.bfloat16)
    for step in range(1, n_blk):
        target = lax.rem(block + step, n_blk)
        copy = pltpu.make_async_remote_copy(
            src_ref=outgoing.at[target],
            dst_ref=incoming.at[step],
            send_sem=scatter_sem.at[step],
            recv_sem=gather_sem.at[step],
            device_id={"blk": target},
            device_id_type=MESH,
        )
        copy.start()
        sends.append(copy)
    total = outgoing[block].astype(jnp.float32)
    for step in range(1, n_blk):
        sends[levels + step - 1].wait_recv()
        total = total + incoming[step].astype(jnp.float32)
    out_ref[0] = (total * (1.0 / math.sqrt(n_blk))).astype(jnp.bfloat16)
    for copy in sends:
        copy.wait_send()


def solution(mesh):
    n_blk, n_bfly = mesh.shape["blk"], mesh.shape["bfly"]

    def local(port_vectors, column_leaf, transfer, row_leaf):
        _, _, leaf, ports = port_vectors.shape
        rank = column_leaf.shape[2]
        levels = transfer.shape[1]
        owned = row_leaf.shape[2] // n_blk
        bf16 = jnp.bfloat16
        return pl.pallas_call(
            functools.partial(kernel, n_blk, n_bfly),
            out_shape=jax.ShapeDtypeStruct((1, owned, ports), bf16),
            in_specs=[pl.BlockSpec(memory_space=pl.ANY)] * 4,
            out_specs=pl.BlockSpec(memory_space=pltpu.VMEM),
            scratch_shapes=[
                pltpu.VMEM((leaf, ports), bf16),
                pltpu.VMEM((rank, leaf), bf16),
                pltpu.VMEM((levels, rank, 2 * rank), bf16),
                pltpu.VMEM((row_leaf.shape[2], rank), bf16),
                pltpu.VMEM((levels, 2 * rank, ports), bf16),
                pltpu.VMEM((n_blk, owned, ports), bf16),
                pltpu.VMEM((n_blk, owned, ports), bf16),
                pltpu.SemaphoreType.DMA((3 + levels,)),
                pltpu.SemaphoreType.DMA((levels,)),
                pltpu.SemaphoreType.DMA((levels,)),
                pltpu.SemaphoreType.DMA((n_blk,)),
                pltpu.SemaphoreType.DMA((n_blk,)),
            ],
            compiler_params=pltpu.CompilerParams(collective_id=0, has_side_effects=True),
        )(port_vectors, column_leaf, transfer, row_leaf)

    placed = (
        P("blk", "bfly", None, None),
        P("blk", "bfly", None, None),
        P("blk", None, "bfly", None, None),
        P("blk", "bfly", None, None),
    )
    return jax.shard_map(
        local, mesh=mesh, in_specs=placed, out_specs=P("bfly", "blk", None), check_vma=False
    )
```

time: 98.6 us -> 24.8 us (0.25)
  waiting for transfers between devices: 71.7 us -> 0 us
  Pallas kernels: 0 us -> 23.3 us
  between operations: 13.5 us -> 0.01 us
  starting transfers between devices: 5.02 us -> 0 us
  matrix products: 3.82 us -> 0 us
  local copies, waits for them, and re-layouts: 4.27 us -> 1.35 us
    unnamed x2 -> x0, waiting for transfers between devices: 63.9 us -> none
    pallas_call x0 -> x1, Pallas kernels: none -> 23.3 us  [local(): pl.pallas_call(functools.partial(kernel, n_blk, n_bfly), out_shape=jax.Sh...]
    ppermute x4 -> x0, waiting for transfers between devices: 7.86 us -> none  [from_partner(): lax.ppermute(array, axis, [(i, i ^ 1 << bit) for i in range(lax.axis_size...]
    ppermute x4 -> x0, starting transfers between devices: 5.02 us -> none  [from_partner(): lax.ppermute(array, axis, [(i, i ^ 1 << bit) for i in range(lax.axis_size...]
    dot_general x9 -> x0, matrix products: 3.82 us -> none  [the longest x1 1.48 us: local(): jnp.dot(column_leaf[0, 0], port_vectors[0, 0], preferred_element_type=jnp...]
    squeeze x1 -> x0, local copies, waits for them, and re-layouts: 1.75 us -> none  [local(): matrix = transfer[0, level, 0]]
  transfers between devices with their start and end apart: 5 -> 0, of which waited for: 4 -> 0; matrix products, arithmetic and copies ran while one was open for 2% -> 0% of each run, Pallas kernels for 0% -> 0%
where the time goes in v1:
time: 24.8 us; the launch traced here: 24.6 us
  Pallas kernels  23.3 us (94%)
  local copies, waits for them, and re-layouts  1.35 us (5%)
    pallas_call x1, Pallas kernels, local(): pl.pallas_call(functools.partial(kernel, n_blk, n_bfly), out_shape=jax.Sh...  23.3 us
    unnamed x1, local copies, waits for them, and re-layouts  1.35 us

profile of v1, /device:TPU:0, one launch (start us, length us, event | category | flops | bytes accessed | tf_op | source)
XLA Modules:
  0.0 24.6 jit_solution(11997352603194483922)
XLA Ops:
  0.0 23.3 %shard_map.46 = bf16[1,96,128]{2,1,0:T(8,128)(2,1)} custom-call(bf16[1,1,768,128]{3,2,1,0:T(8,128)(2,1)} %ports_hbm.1, bf16[1,1,384,768]{3,2,1,0:T(8,128)(2,1)} %column_hbm.1, bf16[1,4,1,384,768]{4,3,2,1,0:T(8,128)(2,1)} %transfer_hbm.1, bf16[1,1,768,384]{3,2,1,0:T(8,128)(2,1)} %row_hbm.1), custom_call_target="tpu_custom_call" | custom-call | tf_op jit(solution)/shard_map/pallas_call | solution.py:119
  23.3 1.3 %copy.6 = bf16[1,96,128]{2,1,0:T(8,128)(2,1)} copy(bf16[1,96,128]{2,1,0:T(8,128)(2,1)} %shard_map.46) | data formatting | bytes 49152

commit v2 on v1

--- a/solution.py
+++ b/solution.py
@@ -8,13 +8,14 @@
 from jax.experimental.pallas import tpu as pltpu
 from jax.sharding import PartitionSpec as P
 
+PIECES = 2
 MESH = pl.DeviceIdType.MESH
 
 
 def kernel(
-    n_blk, n_bfly,
+    n_blk, n_bfly, pieces,
     ports_hbm, column_hbm, transfer_hbm, row_hbm, out_ref,
-    ports, column, transfer, row, stacked, outgoing, incoming,
+    ports, column, transfer, row, stacked, outgoing, incoming, merged, partial,
     load_sem, send_sem, recv_sem, scatter_sem, gather_sem,
 ):
     levels, rank, _ = transfer.shape
@@ -55,37 +56,70 @@
     pl.semaphore_wait(barrier, min(bit_count, levels) + n_blk - 1)
 
     sends = []
-    for level in range(levels):
-        bit = level % bit_count
-        mine = pl.ds(pl.multiple_of(bits[bit] * rank, rank), rank)
-        other = pl.ds(pl.multiple_of((1 - bits[bit]) * rank, rank), rank)
-        stacked[level, mine, :] = state.astype(jnp.bfloat16)
+    width = ports.shape[1] // pieces
+    spans = [pl.ds(piece * width, width) for piece in range(pieces)]
+
+    def side(which):
+        return pl.ds(pl.multiple_of(which * rank, rank), rank)
+
+    def send(level, piece, value):
+        mine = bits[level % bit_count]
+        stacked[level, mine, spans[piece], :] = value.astype(jnp.bfloat16)
         copy = pltpu.make_async_remote_copy(
-            src_ref=stacked.at[level, mine, :],
-            dst_ref=stacked.at[level, mine, :],
-            send_sem=send_sem.at[level],
-            recv_sem=recv_sem.at[level],
-            device_id={"bfly": partners[bit]},
+            src_ref=stacked.at[level, mine, spans[piece], :],
+            dst_ref=stacked.at[level, mine, spans[piece], :],
+            send_sem=send_sem.at[level, piece],
+            recv_sem=recv_sem.at[level, piece],
+            device_id={"bfly": partners[level % bit_count]},
             device_id_type=MESH,
         )
         copy.start()
         sends.append(copy)
-        loads[2 + level].wait()
-        state = jnp.dot(
-            transfer[level, :, mine], stacked[level, mine, :],
-            preferred_element_type=jnp.float32,
-        )
-        copy.wait_recv()
-        state = state + jnp.dot(
-            transfer[level, :, other], stacked[level, other, :],
-            preferred_element_type=jnp.float32,
+        return copy
+
+    def mix(level, which, piece):
+        return lax.dot_general(
+            stacked[level, which, spans[piece], :], transfer[level, :, side(which)],
+            (((1,), (1,)), ((), ())), preferred_element_type=jnp.float32,
         )
 
-    loads[2 + levels].wait()
-    state = state.astype(jnp.bfloat16)
-    partial = jnp.dot(row[...], state, preferred_element_type=jnp.float32)
+    def rows(which):
+        return lax.dot_general(
+            merged[:, side(which)], stacked[levels - 1, which],
+            (((1,), (1,)), ((), ())), preferred_element_type=jnp.float32,
+        )
+
+    first = state.T
+    flying = [
+        send(0, piece, first[piece * width : (piece + 1) * width]) for piece in range(pieces)
+    ]
+    for level in range(levels - 1):
+        mine = bits[level % bit_count]
+        if level == 0:
+            loads[2].wait()
+            begun = [mix(0, mine, piece) for piece in range(pieces)]
+        loads[3 + level].wait()
+        following, later = [], []
+        for piece in range(pieces):
+            flying[piece].wait_recv()
+            mixed = begun[piece] + mix(level, 1 - mine, piece)
+            following.append(send(level + 1, piece, mixed))
+            if level + 1 < levels - 1:
+                later.append(mix(level + 1, bits[(level + 1) % bit_count], piece))
+        flying, begun = following, later
+        if level == min(1, levels - 2):
+            loads[2 + levels].wait()
+    level = levels - 1
+    mine = bits[level % bit_count]
+    merged[...] = jnp.dot(
+        row[...], transfer[level], preferred_element_type=jnp.float32
+    ).astype(jnp.bfloat16)
+    partial[...] = rows(mine)
+    for copy in flying:
+        copy.wait_recv()
+    total = partial[...] + rows(1 - mine)
     for index in range(n_blk):
-        outgoing[index] = partial[index * owned : (index + 1) * owned].astype(jnp.bfloat16)
+        outgoing[index] = total[index * owned : (index + 1) * owned].astype(jnp.bfloat16)
     for step in range(1, n_blk):
         target = lax.rem(block + step, n_blk)
         copy = pltpu.make_async_remote_copy(
@@ -100,7 +134,7 @@
         sends.append(copy)
     total = outgoing[block].astype(jnp.float32)
     for step in range(1, n_blk):
-        sends[levels + step - 1].wait_recv()
+        sends[levels * pieces + step - 1].wait_recv()
         total = total + incoming[step].astype(jnp.float32)
     out_ref[0] = (total * (1.0 / math.sqrt(n_blk))).astype(jnp.bfloat16)
     for copy in sends:
@@ -117,8 +151,8 @@
         owned = row_leaf.shape[2] // n_blk
         bf16 = jnp.bfloat16
         return pl.pallas_call(
-            functools.partial(kernel, n_blk, n_bfly),
-            out_shape=jax.ShapeDtypeStruct((1, owned, ports), bf16),
+            functools.partial(kernel, n_blk, n_bfly, PIECES),
+            out_shape=pltpu.VMEM((1, owned, ports), bf16),
             in_specs=[pl.BlockSpec(memory_space=pl.ANY)] * 4,
             out_specs=pl.BlockSpec(memory_space=pltpu.VMEM),
             scratch_shapes=[
@@ -126,12 +160,14 @@
                 pltpu.VMEM((rank, leaf), bf16),
                 pltpu.VMEM((levels, rank, 2 * rank), bf16),
                 pltpu.VMEM((row_leaf.shape[2], rank), bf16),
-                pltpu.VMEM((levels, 2 * rank, ports), bf16),
+                pltpu.VMEM((levels, 2, ports, rank), bf16),
                 pltpu.VMEM((n_blk, owned, ports), bf16),
                 pltpu.VMEM((n_blk, owned, ports), bf16),
+                pltpu.VMEM((row_leaf.shape[2], 2 * rank), bf16),
+                pltpu.VMEM((row_leaf.shape[2], ports), jnp.float32),
                 pltpu.SemaphoreType.DMA((3 + levels,)),
-                pltpu.SemaphoreType.DMA((levels,)),
-                pltpu.SemaphoreType.DMA((levels,)),
+                pltpu.SemaphoreType.DMA((levels, PIECES)),
+                pltpu.SemaphoreType.DMA((levels, PIECES)),
                 pltpu.SemaphoreType.DMA((n_blk,)),
                 pltpu.SemaphoreType.DMA((n_blk,)),
             ],

time: 24.8 us -> 22.3 us (0.90)
  Pallas kernels: 23.3 us -> 21.5 us
  local copies, waits for them, and re-layouts: 1.35 us -> 0.61 us
    pallas_call x1, Pallas kernels: 23.3 us -> 21.5 us  [local(): pl.pallas_call(functools.partial(kernel, n_blk, n_bfly, PIECES), out_shap...]
    unnamed x1, local copies, waits for them, and re-layouts: 1.35 us -> 0.61 us
where the time goes in v2:
time: 22.3 us; the launch traced here: 22.1 us
  Pallas kernels  21.5 us (96%)
  local copies, waits for them, and re-layouts  0.61 us (3%)
    pallas_call x1, Pallas kernels, local(): pl.pallas_call(functools.partial(kernel, n_blk, n_bfly, PIECES), out_shap...  21.5 us
    unnamed x1, local copies, waits for them, and re-layouts  0.61 us

profile of v2, /device:TPU:0, one launch (start us, length us, event | category | flops | bytes accessed | tf_op | source)
XLA Modules:
  0.0 22.1 jit_solution(2216621216480003046)
XLA Ops:
  0.0 21.5 %shard_map.46 = bf16[1,96,128]{2,1,0:T(8,128)(2,1)S(1)} custom-call(bf16[1,1,768,128]{3,2,1,0:T(8,128)(2,1)} %ports_hbm.1, bf16[1,1,384,768]{3,2,1,0:T(8,128)(2,1)} %column_hbm.1, bf16[1,4,1,384,768]{4,3,2,1,0:T(8,128)(2,1)} %transfer_hbm.1, bf16[1,1,768,384]{3,2,1,0:T(8,128)(2,1)} %row_hbm.1), custom_call_target="tpu_custom_call" | custom-call | tf_op jit(solution)/shard_map/pallas_call | solution.py:153
  21.5 0.6 %copy.6 = bf16[1,96,128]{2,1,0:T(8,128)(2,1)} copy(bf16[1,96,128]{2,1,0:T(8,128)(2,1)S(1)} %shard_map.46) | data formatting | bytes 49152
